TPU v7x, 256 devices: a whole 4x4x8 slice. The times are simulated.
256 devices in a mesh: dp: 32 (over z_lo, x, core), mp: 8 (over z_hi, y).
Axes of the slice: x: 4, y: 4, z: 8 (z_hi: 2, z_lo: 4; z = z_hi * 4 + z_lo), core: 2. Of those that a mesh axis runs over, the one named last changes fastest.
Arguments:
- queries: bfloat16 [24576, 1024], P('dp', 'mp'), may hold values from -3 to 3
- passages: bfloat16 [24576, 1024], P('dp', 'mp'), may hold values from -3 to 3
- positive: int32 [24576], P('dp'), may hold values from 0 to 24575
Outputs:
- grad_queries: bfloat16 [24576, 1024], P('dp', 'mp')
- grad_passages: bfloat16 [24576, 1024], P('dp', 'mp')
All inputs are finite; a program needn't handle non-finite values.
Results may differ from a plain program's by a relative error of at most 0.0034.
Values may be sent and summed in bfloat16 or wider, within the bound.
A program may use at most 128 MiB of HBM per device.

v0:
```python
import math

import jax
import jax.numpy as jnp
from jax import lax
from jax.sharding import Mesh
from jax.sharding import PartitionSpec as P

MP = ("mp_0", "mp_1")


def sent_to_all(array, axis):
    copies = jnp.broadcast_to(array, (lax.axis_size(axis), *array.shape))
    return lax.all_to_all(copies, axis, split_axis=0, concat_axis=0, tiled=True)


def collected_together(array, axis):
    leaves = jax.tree.leaves(array)
    turns = sorted(range(len(leaves)), key=lambda k: -leaves[k].size)
    width = (1, *leaves[turns[0]].shape)[-1]
    lines = [
        jnp.pad(leaves[k].reshape(-1), (0, -leaves[k].size % width)).reshape(-1, width)
        for k in turns
    ]
    both, at, found = (sent_to_all(jnp.concatenate(lines), axis), 0, {})
    for k, line in zip(turns, lines):
        slab = both[:, at : at + len(line)].reshape(len(both), -1)
        found[k] = slab[:, : leaves[k].size].reshape(-1, *leaves[k].shape)
        at += len(line)
    numbers = iter(range(len(leaves)))
    return jax.tree.map(lambda _: found[next(numbers)], array)


def joined_by_halves(pieces, combine):
    while len(jax.tree.leaves(pieces)[0]) > 1:
        pieces = jax.vmap(combine)(
            *(jax.tree.map(lambda part: part[side::2], pieces) for side in (0, 1))
        )
    return jax.tree.map(lambda part: part[0], pieces)


def joined_all(array, axis, combine):
    pieces = collected_together(array, axis)
    return joined_by_halves(pieces, combine)


def sum_in_order(pieces, axes, turns):
    shape = [lax.axis_size(a) for a in axes]
    pieces = pieces.reshape(*shape, *pieces.shape[1:])
    pieces = pieces.transpose(*turns, *range(len(axes), pieces.ndim))
    pieces = pieces.reshape(-1, *pieces.shape[len(axes) :])
    for k in turns:
        pieces = lax.psum_scatter(pieces, axes[k], scatter_dimension=0, tiled=True)
    return pieces[0]


def in_blocks(array, dim, count):
    before, after = (array.shape[:dim], array.shape[dim + 1 :])
    return jnp.moveaxis(array.reshape(*before, count, -1, *after), dim, 0)


def scatter_axes(array, axes, turns, dim):
    count = lax.axis_size(axes)
    return sum_in_order(in_blocks(array, dim, count), axes, turns)


def combine(first, second):
    highest = jnp.maximum(first[0], second[0])
    merged = first[1] * jnp.exp(first[0] - highest) + second[1] * jnp.exp(second[0] - highest)
    return (highest, merged)


def local(queries, passages, positive):
    group_rows, slice_width = queries.shape
    group_count = lax.axis_size("dp")
    model_index = lax.axis_index(MP)
    relaid = lax.all_to_all(passages, MP, split_axis=0, concat_axis=1, tiled=True)
    short_rows = relaid.shape[0]
    wide_queries = lax.all_gather(queries, MP, axis=1, tiled=True)
    passage_block = lax.all_gather(relaid, "dp", axis=0, tiled=True)
    full_width = wide_queries.shape[1]
    logit_scale = 3.0 / math.sqrt(full_width)
    scores = (
        lax.dot_general(
            wide_queries,
            passage_block,
            (((1,), (1,)), ((), ())),
            preferred_element_type=jnp.float32,
        )
        * logit_scale
    )
    local_max = jnp.max(scores, axis=1)
    local_total = jnp.sum(jnp.exp(scores - local_max[:, None]), axis=1)
    highest, row_total = joined_all((local_max, local_total), MP, combine)
    log_total = highest + jnp.log(row_total)
    column_pos = jnp.arange(group_count * short_rows, dtype=jnp.int32)
    column_ids = (
        column_pos // short_rows * group_rows + model_index * short_rows + column_pos % short_rows
    )
    onehot = (column_ids[None, :] == positive[:, None]).astype(jnp.float32)
    softmax_grad = (jnp.exp(scores - log_total[:, None]) - onehot).astype(jnp.bfloat16)
    query_terms = jnp.dot(softmax_grad, passage_block, preferred_element_type=jnp.float32)
    grad_queries = scatter_axes(query_terms, MP, (1, 0), 1).astype(jnp.bfloat16)
    summed = lax.psum_scatter(
        lax.dot_general(
            softmax_grad, wide_queries, (((0,), (0,)), ((), ())), preferred_element_type=jnp.float32
        ),
        "dp",
        scatter_dimension=0,
        tiled=True,
    )
    grad_passages = lax.all_to_all(
        summed.astype(jnp.bfloat16), MP, split_axis=1, concat_axis=0, tiled=True
    )
    return (grad_queries, grad_passages)


def solution(mesh):
    finer = Mesh(mesh.devices.reshape(mesh.shape["dp"], 2, 4), ("dp", "mp_0", "mp_1"))
    return jax.shard_map(
        local,
        mesh=finer,
        in_specs=(P("dp", MP), P("dp", MP), P("dp")),
        out_specs=(P("dp", MP), P("dp", MP)),
        check_vma=False,
    )
```

profile of v0, /device:TPU:8, one launch (start us, length us, event | category | flops | bytes accessed | tf_op | source)
XLA Modules:
  0.0 440.7 jit_solution(9130345755610493085)
XLA Ops:
  7.2 0.0 all-gather.3.cloned.1.call-start
  7.2 0.7 all-gather.3.cloned.1.call-update
  7.9 0.0 all-gather.5.cloned.1.call-start
  7.9 20.7 %all_to_all.43 = bf16[8,96,128]{2,1,0:T(8,128)(2,1)S(1)} all-to-all(bf16[8,96,128]{2,1,0:T(8,128)(2,1)} %bitcast.38), channel_id=1, replica_groups=mesh['dp'=32,'mp_0'=2,'mp_1'=4] {'mp_0','mp_1'}, dimensions={0} | all-to-all | bytes 393216 | tf_op jit(solution)/shard_map/all_to_all | solution.py:77
  28.7 0.7 copy_bitcast_fusion
  29.3 0.0 all-gather.5.cloned.1.call-update
  29.4 52.3 %all-gather.3.cloned.1.call-done = bf16[768,1024]{1,0:T(8,128)(2,1)} async-done(((bf16[768,128]{1,0:T(8,128)(2,1)}), bf16[768,1024]{1,0:T(8,128)(2,1)}) %all-gather.3.cloned.1.call-update) | async-done | bytes 1572880 | tf_op jit(solution)/shard_map/all_gather | solution.py:79
  81.6 65.0 %all-gather.5.cloned.1.call-done = bf16[3072,1024]{1,0:T(8,128)(2,1)} async-done(((bf16[96,1024]{1,0:T(8,128)(2,1)}), bf16[3072,1024]{1,0:T(8,128)(2,1)}) %all-gather.5.cloned.1.call-update) | async-done | bytes 6291472 | tf_op jit(solution)/shard_map/all_gather | solution.py:80
  146.7 7.8 %multiply_reduce_fusion = (f32[768]{0:T(1024)S(1)}, f32[768,3072]{1,0:T(8,128)S(1)}) fusion(bf16[768,1024]{1,0:T(8,128)(2,1)} %all-gather.3.cloned.1.call-done, bf16[3072,1024]{1,0:T(8,128)(2,1)} %all-gather.5.cloned.1.call-done), kind=kOutput, calls=%fused_computation.2 | convolution fusion | flops 4836555776 | bytes 17304576 | tf_op jit(solution)/shard_map/dot_general | solution.py:84
  154.5 0.0 copy-start
  154.5 0.0 copy-start.2
  154.5 3.5 copy-done
  158.0 1.7 exponential_reduce_fusion
  159.7 0.6 broadcast_in_dim.2
  160.3 8.7 %all-to-all-start.1 = ((f32[8,2,768]{2,1,0:T(2,128)}), f32[8,2,768]{2,1,0:T(2,128)S(1)}, u32[]{:S(2)}, u32[]{:S(2)}) async-start(f32[8,2,768]{2,1,0:T(2,128)} %broadcast_in_dim.2), calls=%async_computation.1 | async-start | bytes 98304 | tf_op jit(solution)/shard_map/all_to_all | solution.py:14
  169.0 0.0 reduce-scatter.4.cloned.1.call-start
  169.0 8.7 %all-to-all-done.1 = f32[8,2,768]{2,1,0:T(2,128)S(1)} async-done(((f32[8,2,768]{2,1,0:T(2,128)}), f32[8,2,768]{2,1,0:T(2,128)S(1)}, u32[]{:S(2)}, u32[]{:S(2)}) %all-to-all-start.1) | async-done | bytes 49184 | tf_op jit(solution)/shard_map/all_to_all | solution.py:14
  178.1 0.0 copy-done.2
  178.1 9.8 %convolution_bitcast_fusion = f32[96,8,8,128]{3,1,2,0:T(8,128)S(1)} fusion(bf16[3072,1024]{1,0:T(8,128)(2,1)} %all-gather.5.cloned.1.call-done, f32[768,3072]{1,0:T(8,128)} %copy-done, s32[3072]{0:T(1024)S(1)} %fusion.8, f32[768]{0:T(1024)S(1)} %add_reduce_fusion, s32[768]{0:T(1024)S(1)} %copy-done.2), kind=kOutput, calls=%fused_computation.3 | convolution fusion | flops 4845993984 | bytes 18892800 | tf_op jit(solution)/shard_map/dot_general | solution.py:102
  188.0 0.0 copy-start.1
  188.0 0.7 copy.20
  188.7 2.2 copy.14
  191.0 0.0 reduce-scatter.4.cloned.1.call-update
  191.0 0.0 reduce-scatter.8.cloned.1.call-start
  191.0 0.0 copy-done.1
  191.0 11.1 %fusion.12 = f32[3072,1024]{1,0:T(8,128)} fusion(bf16[768,1024]{1,0:T(8,128)(2,1)S(1)} %copy-done.1, f32[768,3072]{1,0:T(8,128)} %copy-done, s32[3072]{0:T(1024)S(1)} %fusion.8, f32[768]{0:T(1024)S(1)} %add_reduce_fusion, s32[768]{0:T(1024)S(1)} %copy-done.2), kind=kOutput, calls=%fused_computation.33 | convolution fusion | flops 4845993984 | bytes 23611392 | tf_op jit(solution)/shard_map/dot_general | solution.py:105
  202.1 0.0 reduce-scatter.8.cloned.1.call-update
  202.1 0.0 reduce-scatter.6.cloned.1.call-start
  202.2 23.9 %reduce-scatter.4.cloned.1.call-done = f32[2,768,128]{2,1,0:T(8,128)} async-done(((f32[8,768,128]{2,1,0:T(8,128)}), f32[2,768,128]{2,1,0:T(8,128)}) %reduce-scatter.4.cloned.1.call-update) | async-done | bytes 786448 | tf_op jit(solution)/shard_map/reduce_scatter | solution.py:53
  226.1 0.0 reduce-scatter.6.cloned.1.call-update
  226.2 171.3 %reduce-scatter.8.cloned.1.call-done = f32[96,1024]{1,0:T(8,128)} async-done(((f32[3072,1024]{1,0:T(8,128)}), f32[96,1024]{1,0:T(8,128)}) %reduce-scatter.8.cloned.1.call-update) | async-done | bytes 393232 | tf_op jit(solution)/shard_map/reduce_scatter | solution.py:104
  397.5 1.7 copy_bitcast_fusion.1
  399.2 6.7 %all-to-all-start.2 = ((bf16[96,8,128]{2,0,1:T(8,128)(2,1)}), bf16[96,8,128]{2,0,1:T(8,128)(2,1)S(1)}, u32[]{:S(2)}, u32[]{:S(2)}) async-start(bf16[96,8,128]{2,0,1:T(8,128)(2,1)} %copy_bitcast_fusion.1), calls=%async_computation.5 | async-start | bytes 393216 | tf_op jit(solution)/shard_map/all_to_all | solution.py:112
  405.8 26.0 %reduce-scatter.6.cloned.1.call-done = f32[1,768,128]{2,1,0:T(8,128)} async-done(((f32[2,768,128]{2,1,0:T(8,128)}), f32[1,768,128]{2,1,0:T(8,128)}) %reduce-scatter.6.cloned.1.call-update) | async-done | bytes 393232 | tf_op jit(solution)/shard_map/reduce_scatter | solution.py:53
  431.8 1.7 convert_bitcast_fusion.1
  433.5 0.0 all-to-all-done.2
  433.5 0.7 copy.26
  (17 shorter events, 0.4 us)
Async XLA Ops:
  7.2 74.5 %all-gather.3.cloned.1.call-start = ((), (), s32[]{:S(2)}) async-start(), calls=%async_computation.6 | async-start | bytes 1769472 | tf_op jit(solution)/shard_map/all_gather | solution.py:79
  7.9 138.8 %all-gather.5.cloned.1.call-start = ((), (), s32[]{:S(2)}) async-start(), calls=%async_computation.7 | async-start | bytes 6488064 | tf_op jit(solution)/shard_map/all_gather | solution.py:80
  154.5 3.5 copy-start
  154.5 23.6 %copy-start.2 = (s32[768]{0:T(1024)S(1)}, s32[768]{0:T(1024)}, u32[]{:S(2)}) copy-start(s32[768]{0:T(1024)} %param.5) | copy-start | bytes 9220
  160.3 17.4 %all-to-all-start.1 = ((f32[8,2,768]{2,1,0:T(2,128)}), f32[8,2,768]{2,1,0:T(2,128)S(1)}, u32[]{:S(2)}, u32[]{:S(2)}) async-start(f32[8,2,768]{2,1,0:T(2,128)} %broadcast_in_dim.2), calls=%async_computation.1 | async-start | bytes 98304 | tf_op jit(solution)/shard_map/all_to_all | solution.py:14
  169.0 57.1 %reduce-scatter.4.cloned.1.call-start = ((), (), s32[]{:S(2)}) async-start(), calls=%async_computation.8 | async-start | bytes 3932160 | tf_op jit(solution)/shard_map/reduce_scatter | solution.py:53
  188.0 3.1 copy-start.1
  191.0 206.5 %reduce-scatter.8.cloned.1.call-start = ((), (), s32[]{:S(2)}) async-start(), calls=%async_computation.10 | async-start | bytes 12976128 | tf_op jit(solution)/shard_map/reduce_scatter | solution.py:104
  202.1 229.6 %reduce-scatter.6.cloned.1.call-start = ((), (), s32[]{:S(2)}) async-start(), calls=%async_computation.9 | async-start | bytes 1179648 | tf_op jit(solution)/shard_map/reduce_scatter | solution.py:53
  399.2 34.3 %all-to-all-start.2 = ((bf16[96,8,128]{2,0,1:T(8,128)(2,1)}), bf16[96,8,128]{2,0,1:T(8,128)(2,1)S(1)}, u32[]{:S(2)}, u32[]{:S(2)}) async-start(bf16[96,8,128]{2,0,1:T(8,128)(2,1)} %copy_bitcast_fusion.1), calls=%async_computation.5 | async-start | bytes 393216 | tf_op jit(solution)/shard_map/all_to_all | solution.py:112
Sparse Core Ops, SparseCore 0:
  10.4 71.1 all-gather.2
  84.1 62.5 all-gather.4
  191.1 34.9 reduce-scatter.3
  228.5 168.8 reduce-scatter.7
  399.8 31.9 reduce-scatter.5
where the time goes:
time: 442 us; the launch traced here: 441 us
  waiting for transfers between devices  348 us (79%)
  matrix products  28.7 us (6%)
  blocking collectives  20.7 us (5%)
  starting transfers between devices  15.5 us (4%)
  between operations  13.9 us (3%)
  local copies, waits for them, and re-layouts  8.76 us (2%)
  other arithmetic  5.15 us (1%)
    reduce_scatter x1, waiting for transfers between devices, local(): lax.psum_scatter(lax.dot_general(softmax_grad, wide_queries, (((0,), (0,)...  171 us
    all_gather x1, waiting for transfers between devices, local(): passage_block = lax.all_gather(relaid, 'dp', axis=0, tiled=True)  65 us
    all_gather x1, waiting for transfers between devices, local(): wide_queries = lax.all_gather(queries, MP, axis=1, tiled=True)  52.3 us
    reduce_scatter x2, waiting for transfers between devices, sum_in_order(): pieces = lax.psum_scatter(pieces, axes[k], scatter_dimension=0, tiled=True)  49.9 us
    all_to_all x1, blocking collectives, local(): lax.all_to_all(passages, MP, split_axis=0, concat_axis=1, tiled=True)  20.7 us
    dot_general x1, matrix products, local(): lax.dot_general(softmax_grad, wide_queries, (((0,), (0,)), ((), ())), pre...  11.1 us
    dot_general x1, matrix products, local(): jnp.dot(softmax_grad, passage_block, preferred_element_type=jnp.float32)  9.82 us
  transfers between devices with their start and end apart: 7, of which 6 were waited for; matrix products, arithmetic and copies ran while one was open for 3% of the time, Pallas kernels for 0%

commit v1 on v0

v1 whole, which is shorter than its diff:
```python
import functools
import math

import jax
import jax.numpy as jnp
from jax import lax
from jax.experimental import pallas as pl
from jax.experimental.pallas import tpu as pltpu
from jax.sharding import Mesh
from jax.sharding import PartitionSpec as P

BF16, F32 = jnp.bfloat16, jnp.float32
D = 1024
SCALE = 3.0 / math.sqrt(D)
QUARTER, HALF = 192, 384
BLOCK = 1536
GROUP = 768
COPIES = 208
NT = (((1,), (1,)), ((), ()))
TN = (((0,), (0,)), ((), ()))


def place(dx=0, dy=0, dz=0, dc=0):
    z = lax.rem(lax.axis_index("zh") * 4 + lax.axis_index("zl") + dz + 8, 8)
    return {
        "zl": lax.rem(z, 4),
        "x": lax.rem(lax.axis_index("x") + dx + 4, 4),
        "c": lax.rem(lax.axis_index("c") + dc, 2),
        "zh": lax.div(z, 4),
        "y": lax.rem(lax.axis_index("y") + dy + 4, 4),
    }


def kernel(
    q, p, pos, oq, op,
    qb, pb, posb, sc, sg, st,
    da, db, own_a, own_b, ra, rb, s2a, s2b, r2a, r2b, zs, zr,
    dps, dpr, sf, rf, sy, ry,
    ssem, rsem,
):
    x, y, c, zl, zh = (lax.axis_index(a) for a in ("x", "y", "c", "zl", "zh"))
    oc = 1 - c
    oz = 1 - zh
    sent = []

    def send(src, dst, **where):
        k = len(sent)
        copy = pltpu.make_async_remote_copy(
            src_ref=src, dst_ref=dst, send_sem=ssem.at[k], recv_sem=rsem.at[k],
            device_id=place(**where), device_id_type=pl.DeviceIdType.MESH,
        )
        copy.start()
        sent.append(copy)
        return copy

    def half_of(dz):
        return lax.div(lax.rem(zh * 4 + zl + dz, 8), 4)

    plane = [(dx, dy) for dx in range(4) for dy in range(4) if dx or dy]
    peers = [dict(dx=dx, dy=dy) for dx, dy in plane]
    peers += [dict(dz=1), dict(dz=-1), dict(dz=4), dict(dc=1)]
    barrier = pltpu.get_barrier_semaphore()
    for where in peers:
        pl.semaphore_signal(barrier, inc=1, device_id=place(**where), device_id_type=pl.DeviceIdType.MESH)
    pl.semaphore_wait(barrier, len(peers))

    swap = send(q.at[pl.ds(oz * 2, 2)], qb.at[0, zh, :, pl.ds(0, QUARTER)], dz=4)
    mine = pl.ds(pl.multiple_of(c * QUARTER, 16), QUARTER)
    spread = {}
    for d in (1, 3, 2):
        rows = pl.ds(pl.multiple_of(lax.rem(y + d, 4) * QUARTER, 16), QUARTER)
        spread[-d % 4] = send(p.at[rows], pb.at[-d % 4, zh, mine], dy=d)
    own_rows = pl.ds(pl.multiple_of(zh * HALF, 16), HALF)
    from_y, from_x = {}, {}

    def share(src, h, tag):
        for d in (1, 3, 2):
            from_y[-d % 4, tag] = send(src, qb.at[-d % 4, h, :, pl.ds(0, QUARTER)], dy=d)
            from_x[-d % 4, tag] = send(src, qb.at[0, h, :, pl.ds((-d % 4) * QUARTER, QUARTER)], dx=d)

    share(q.at[pl.ds(zh * 2, 2)], zh, 0)
    from_pos = {d: send(pos.at[zh], posb.at[-d % 4], dx=d) for d in (1, 3, 2)}
    for g in (0, 1):
        qb[0, zh, g, 0:QUARTER, :] = q[zh * 2 + g]
    posb[0] = pos[zh]
    pb[0, zh, mine, :] = p[pl.ds(pl.multiple_of(y * QUARTER, 16), QUARTER), :]

    def piece(dz, sub):
        rows = pl.ds(pl.multiple_of((dz % 4) * 2 * QUARTER + c * QUARTER, 16), QUARTER)
        ys = pl.ds(0, 4) if sub is None else pl.ds(sub * 2, 2)
        return ys, half_of(dz), rows

    ring, cores = {}, {}

    def pass_on(dz, sub, step):
        ys, h, rows = piece(dz, sub)
        to = (dz - step) % 8
        dst_rows = pl.ds(pl.multiple_of((to % 4) * 2 * QUARTER + c * QUARTER, 16), QUARTER)
        ring[to, sub] = send(pb.at[ys, h, rows], pb.at[ys, h, dst_rows], dz=step)

    def to_core(dz):
        ys, h, rows = piece(dz, None)
        cores[dz] = send(pb.at[ys, h, rows], pb.at[ys, h, rows], dc=1)

    spread[1].wait_recv()
    pass_on(0, 0, 1)
    pass_on(0, 0, -1)
    spread[3].wait_recv()
    spread[2].wait_recv()
    pass_on(0, 1, 1)
    pass_on(0, 1, -1)
    to_core(0)
    swap.wait_recv()
    share(qb.at[0, oz, :, pl.ds(0, QUARTER)], oz, 1)

    def hop(n):
        for sub in (0, 1):
            for dz, step in ((n, -1), (8 - n, 1)):
                ring[dz, sub].wait_recv()
                if n < 3 or (sub == 0) == (step == -1):
                    pass_on(dz, sub, step)
        to_core(n)
        to_core(8 - n)

    hop(1)
    second = []
    for k in (1, 3, 2):
        for tag in (0, 1):
            from_y[k, tag].wait_recv()
        for d in (1, 3, 2):
            ref = qb.at[k, :, 0, pl.ds(0, QUARTER)]
            second.append(send(ref, qb.at[k, :, 0, pl.ds((-d % 4) * QUARTER, QUARTER)], dx=d))
        for tag in (0, 1):
            from_x[k, tag].wait_recv()
        for d in (1, 3, 2):
            ref = qb.at[0, :, 1, pl.ds(k * QUARTER, QUARTER)]
            second.append(send(ref, qb.at[-d % 4, :, 1, pl.ds(k * QUARTER, QUARTER)], dy=d))
    hop(2)
    hop(3)
    for sub in (0, 1):
        ring[4, sub].wait_recv()
    to_core(4)
    for copy in second:
        copy.wait_recv()
    for copy in from_pos.values():
        copy.wait_recv()
    for dz in range(8):
        cores[dz].wait_recv()

    def wide(ref, *at):
        return jnp.concatenate([ref[(k, h, *at)] for k in range(4) for h in range(2)], axis=1)

    stats = {}
    for g in (0, 1):

        def scores(j, carry, g=g):
            top, total = carry
            rows = pl.ds(pl.multiple_of(j * HALF, 16), HALF)
            s = lax.dot_general(wide(pb, rows), wide(qb, g), NT, preferred_element_type=F32) * SCALE
            sc[g, rows, :] = s
            higher = jnp.maximum(top, jnp.max(s, axis=0, keepdims=True))
            total = total * jnp.exp(top - higher) + jnp.sum(jnp.exp(s - higher), axis=0, keepdims=True)
            return higher, total

        start = (jnp.full((1, GROUP), -3e38, F32), jnp.zeros((1, GROUP), F32))
        top, total = lax.fori_loop(0, 4, scores, start)
        for i in range(4):
            st[g, 0, i, 0:1, :] = top[:, i * QUARTER : (i + 1) * QUARTER]
            st[g, 0, i, 1:2, :] = total[:, i * QUARTER : (i + 1) * QUARTER]
        for dx, dy in plane:
            stats[g, dx, dy] = send(st.at[g, 0], st.at[g, (-dx % 4) * 4 + (-dy % 4)], dx=dx, dy=dy)

    stage_a, stage_b = {}, {}
    for g in (0, 1):
        for dx, dy in plane:
            stats[g, dx, dy].wait_recv()
        logs = []
        for i in range(4):
            pairs = [(k, (i - k // 4) % 4) for k in range(16)]
            tops = [st[g, k, n, 0:1, :] for k, n in pairs]
            high = functools.reduce(jnp.maximum, tops)
            total = sum(st[g, k, n, 1:2, :] * jnp.exp(t - high) for (k, n), t in zip(pairs, tops))
            logs.append(high + jnp.log(total))
        log_total = jnp.concatenate(logs, axis=1)
        targets = jnp.concatenate([posb[i, g] for i in range(4)], axis=1)

        def normal(j, carry, g=g, log_total=log_total, targets=targets):
            rows = pl.ds(pl.multiple_of(j * QUARTER, 16), QUARTER)
            owner = (lax.rem(zl + lax.div(j, 2), 4) * 4 + x) * 2 + lax.rem(j, 2)
            ids = lax.broadcasted_iota(jnp.int32, (QUARTER, GROUP), 0) + (owner * 768 + y * QUARTER)
            e = jnp.exp(sc[g, rows, :] - log_total)
            sg[g, rows, :] = jnp.where(ids == targets, e - 1.0, e).astype(BF16)
            return carry

        lax.fori_loop(0, 8, normal, 0)
        for k in (1, 3, 2, 0):
            rhs = jnp.concatenate([pb[k, 0], pb[k, 1]], axis=1)
            r = lax.dot_general(sg[g], rhs, TN, preferred_element_type=F32)
            if g == 0:
                own_a[k] = r[:QUARTER]
                for i in (1, 3, 2):
                    da[i, k] = r[i * QUARTER : (i + 1) * QUARTER].astype(BF16)
                    stage_a[-i % 4, k] = send(da.at[i, k], ra.at[-i % 4, k], dx=i)
            elif k:
                db[k] = r.astype(BF16)
                stage_b[-k % 4] = send(db.at[k], rb.at[-k % 4], dy=k)
            else:
                own_b[...] = r

    halves = {}

    def passages(s):
        def columns(k, carry):
            rows = slice(s * HALF, (s + 1) * HALF)
            r = sum(
                jnp.dot(
                    sg[g, rows, :],
                    jnp.concatenate([qb[k, h, g] for h in range(2)], axis=1),
                    preferred_element_type=F32,
                )
                for g in (0, 1)
            )
            for i in range(2):
                for h in range(2):
                    dps[s, i, h, k] = r[i * QUARTER : (i + 1) * QUARTER, h * 128 : (h + 1) * 128]
            return carry

        lax.fori_loop(0, 4, columns, 0)
        halves[s] = send(dps.at[s, oc], dpr.at[s], dc=1)

    def both(dz, k):
        h = half_of(dz)
        return dps[dz % 4, c, h, k] + dpr[dz % 4, h, k]

    sums = {}

    def add_on(way, n, sub, arrived):
        dz = (4 - n) if way == 0 else (4 + n)
        for i in range(2):
            v = both(dz, sub * 2 + i)
            if arrived:
                v = v + rf[way, n, sub, i].astype(F32)
            sf[way, n, sub, i] = v.astype(BF16)
        sums[way, n + 1, sub] = send(sf.at[way, n, sub], rf.at[way, n + 1, sub], dz=1 - 2 * way)

    passages(0)
    passages(3)
    halves[0].wait_recv()
    add_on(0, 0, 0, False)
    add_on(1, 0, 1, False)
    passages(1)
    halves[3].wait_recv()
    add_on(0, 1, 1, False)
    passages(2)
    halves[1].wait_recv()
    add_on(1, 1, 0, False)
    sums[0, 1, 0].wait_recv()
    add_on(0, 1, 0, True)
    sums[1, 1, 1].wait_recv()
    add_on(1, 1, 1, True)
    halves[2].wait_recv()

    def step(n):
        for way, sub in ((0, 1), (1, 0), (0, 0), (1, 1)):
            sums[way, n, sub].wait_recv()
            add_on(way, n, sub, True)

    step(2)

    final_a, final_b = {}, {}
    for k in (1, 3, 2, 0):
        for i in (1, 2, 3):
            stage_a[i, k].wait_recv()
        v = own_a[k] + sum(ra[i, k].astype(F32) for i in (1, 2, 3))
        if k:
            s2a[k] = v.astype(BF16)
            final_a[-k % 4] = send(s2a.at[k], r2a.at[-k % 4], dy=k)
        else:
            own_a[0] = v
    step(3)
    for i in (1, 2, 3):
        stage_b[i].wait_recv()
    for k in (1, 3, 2, 0):
        rows = slice(k * QUARTER, (k + 1) * QUARTER)
        v = own_b[rows, :] + sum(rb[i, rows, :].astype(F32) for i in (1, 2, 3))
        if k:
            s2b[k] = v.astype(BF16)
            final_b[-k % 4] = send(s2b.at[k], r2b.at[-k % 4], dx=k)
        else:
            own_b[rows, :] = v
    for k in (1, 2, 3):
        final_a[k].wait_recv()
        final_b[k].wait_recv()
    fa = own_a[0] + sum(r2a[k].astype(F32) for k in (1, 2, 3))
    fb = own_b[0:QUARTER, :] + sum(r2b[k].astype(F32) for k in (1, 2, 3))
    for h in range(2):
        zs[h, 0:QUARTER, :] = fa[:, h * 128 : (h + 1) * 128].astype(BF16)
        zs[h, QUARTER:HALF, :] = fb[:, h * 128 : (h + 1) * 128].astype(BF16)
    last = send(zs.at[oz], zr, dz=4)
    oq[own_rows, :] = zs[zh]

    for way, sub in ((0, 1), (1, 0), (0, 0), (1, 1)):
        sums[way, 4, sub].wait_recv()
    widths = {}
    for k in (1, 3, 2, 0):
        v = both(0, k) + rf[0, 4, k // 2, k % 2].astype(F32) + rf[1, 4, k // 2, k % 2].astype(F32)
        if k:
            sy[k] = v.astype(BF16)
            widths[-k % 4] = send(sy.at[k], ry.at[-k % 4], dy=k)
        else:
            op[pl.ds(pl.multiple_of(y * QUARTER, 16), QUARTER), :] = v.astype(BF16)
    for k in (1, 2, 3):
        widths[k].wait_recv()
        op[pl.ds(pl.multiple_of(lax.rem(y + k, 4) * QUARTER, 16), QUARTER), :] = ry[k]
    last.wait_recv()
    oq[pl.ds(pl.multiple_of(oz * HALF, 16), HALF), :] = zr[...]
    for copy in sent:
        copy.wait_send()


def local(queries, passages, positive):
    vmem = pl.BlockSpec(memory_space=pltpu.VMEM)
    shapes = [
        ((4, 2, 2, GROUP, 128), BF16),
        ((4, 2, BLOCK, 128), BF16),
        ((4, 2, 1, QUARTER), jnp.int32),
        ((2, BLOCK, GROUP), F32),
        ((2, BLOCK, GROUP), BF16),
        ((2, 16, 4, 2, QUARTER), F32),
        ((4, 4, QUARTER, 256), BF16),
        ((4, GROUP, 256), BF16),
        ((4, QUARTER, 256), F32),
        ((GROUP, 256), F32),
        ((4, 4, QUARTER, 256), BF16),
        ((4, GROUP, 256), BF16),
        ((4, QUARTER, 256), BF16),
        ((4, QUARTER, 256), BF16),
        ((4, QUARTER, 256), BF16),
        ((4, QUARTER, 256), BF16),
        ((2, HALF, 128), BF16),
        ((HALF, 128), BF16),
        ((4, 2, 2, 4, QUARTER, 128), F32),
        ((4, 2, 4, QUARTER, 128), F32),
        ((2, 4, 2, 2, QUARTER, 128), BF16),
        ((2, 5, 2, 2, QUARTER, 128), BF16),
        ((4, QUARTER, 128), BF16),
        ((4, QUARTER, 128), BF16),
    ]
    return pl.pallas_call(
        kernel,
        out_shape=(jax.ShapeDtypeStruct((768, 128), BF16), jax.ShapeDtypeStruct((768, 128), BF16)),
        in_specs=[vmem, vmem, vmem],
        out_specs=(vmem, vmem),
        scratch_shapes=[pltpu.VMEM(s, t) for s, t in shapes]
        + [pltpu.SemaphoreType.DMA((COPIES,)), pltpu.SemaphoreType.DMA((COPIES,))],
        compiler_params=pltpu.CompilerParams(
            collective_id=0, has_side_effects=True, vmem_limit_bytes=62 * 2**20
        ),
    )(queries.reshape(4, QUARTER, 128), passages, positive.reshape(2, 2, 1, QUARTER))


def solution(mesh):
    finer = Mesh(mesh.devices.reshape(4, 4, 2, 2, 4), ("zl", "x", "c", "zh", "y"))
    dp, mp = ("zl", "x", "c"), ("zh", "y")
    return jax.shard_map(
        local,
        mesh=finer,
        in_specs=(P(dp, mp), P(dp, mp), P(dp)),
        out_specs=(P(dp, mp), P(dp, mp)),
        check_vma=False,
    )
```

time: 442 us -> 100 us (0.23)
  waiting for transfers between devices: 348 us -> 0 us
  Pallas kernels: 0 us -> 95.7 us
  matrix products: 28.7 us -> 0 us
  blocking collectives: 20.7 us -> 0 us
  starting transfers between devices: 15.5 us -> 0 us
  between operations: 13.9 us -> 0.65 us
  other arithmetic: 5.15 us -> 0 us
  local copies, waits for them, and re-layouts: 8.76 us -> 3.69 us
    reduce_scatter x3 -> x0, waiting for transfers between devices: 221 us -> none  [the longest x1 171 us: local(): lax.psum_scatter(lax.dot_general(softmax_grad, wide_queries, (((0,), (0,)...]
    all_gather x2 -> x0, waiting for transfers between devices: 117 us -> none  [the longest x1 65 us: local(): passage_block = lax.all_gather(relaid, 'dp', axis=0, tiled=True)]
    pallas_call x0 -> x1, Pallas kernels: none -> 95.7 us  [local(): pl.pallas_call(kernel, out_shape=(jax.ShapeDtypeStruct((768, 128), BF16),...]
    dot_general x3 -> x0, matrix products: 28.7 us -> none  [the longest x1 11.1 us: local(): lax.dot_general(softmax_grad, wide_queries, (((0,), (0,)), ((), ())), pre...]
    all_to_all x1 -> x0, blocking collectives: 20.7 us -> none  [local(): lax.all_to_all(passages, MP, split_axis=0, concat_axis=1, tiled=True)]
    all_to_all x2 -> x0, starting transfers between devices: 15.3 us -> none  [the longest x1 8.67 us: sent_to_all(): return lax.all_to_all(copies, axis, split_axis=0, concat_axis=0, tiled=True)]
    all_to_all x2 -> x0, waiting for transfers between devices: 8.74 us -> none  [the longest x1 8.74 us: sent_to_all(): return lax.all_to_all(copies, axis, split_axis=0, concat_axis=0, tiled=True)]
  transfers between devices with their start and end apart: 7 -> 0, of which waited for: 6 -> 0; matrix products, arithmetic and copies ran while one was open for 3% -> 0% of each run, Pallas kernels for 0% -> 0%
where the time goes in v1:
time: 100 us
  Pallas kernels  95.7 us (96%)
  local copies, waits for them, and re-layouts  3.69 us (4%)
    pallas_call x1, Pallas kernels, local(): pl.pallas_call(kernel, out_shape=(jax.ShapeDtypeStruct((768, 128), BF16),...  95.7 us
    unnamed x4, local copies, waits for them, and re-layouts  2.34 us

profile of v1, /device:TPU:8, one launch (start us, length us, event | category | flops | bytes accessed | tf_op | source)
XLA Modules:
  0.0 100.0 jit_solution(1657728758923704837)
XLA Ops:
  0.6 1.4 %reshape.11.pos = s32[2,2,1,192]{3,2,1,0:T(1,128)} reshape(s32[768]{0:T(1024)} %param.5) | data formatting | bytes 6144 | tf_op jit(solution)/shard_map/reshape | solution.py:359
  2.0 95.7 %shard_map.50 = (bf16[768,128]{1,0:T(8,128)(2,1)}, bf16[768,128]{1,0:T(8,128)(2,1)}) custom-call(bf16[4,192,128]{2,1,0:T(8,128)(2,1)} %bitcast.1, bf16[768,128]{1,0:T(8,128)(2,1)} %p.1, s32[2,2,1,192]{3,2,1,0:T(1,128)} %reshape.11.pos), custom_call_target="tpu_custom_call" | custom-call | tf_op jit(solution)/shard_map/pallas_call | solution.py:349
  97.7 0.0 copy-start
  97.7 1.7 %copy.7 = bf16[768,128]{1,0:T(8,128)(2,1)} copy(bf16[768,128]{1,0:T(8,128)(2,1)} %get-tuple-element.4) | data formatting | bytes 393216
  99.3 0.0 copy-done
  99.3 0.7 copy.8
Async XLA Ops:
  97.7 1.7 %copy-start = (bf16[768,128]{1,0:T(8,128)(2,1)S(1)}, bf16[768,128]{1,0:T(8,128)(2,1)}, u32[]{:S(2)}) copy-start(bf16[768,128]{1,0:T(8,128)(2,1)} %get-tuple-element.5) | copy-start | bytes 589828

commit v2 on v1

v2 whole, which is shorter than its diff:
```python
import functools
import math

import jax
import jax.numpy as jnp
from jax import lax
from jax.experimental import pallas as pl
from jax.experimental.pallas import tpu as pltpu
from jax.sharding import Mesh
from jax.sharding import PartitionSpec as P

BF16, F32 = jnp.bfloat16, jnp.float32
D = 1024
SCALE = 3.0 / math.sqrt(D)
EIGHTH, QUARTER, HALF = 96, 192, 384
BLOCK = 1536
GROUP = 768
ARRIVALS, DEPARTURES = 73, 25
NT = (((1,), (1,)), ((), ()))
TN = (((0,), (0,)), ((), ()))


def place(dx=0, dy=0, dz=0, dc=0):
    z = lax.rem(lax.axis_index("zh") * 4 + lax.axis_index("zl") + dz + 8, 8)
    return {
        "zl": lax.rem(z, 4),
        "x": lax.rem(lax.axis_index("x") + dx + 4, 4),
        "c": lax.rem(lax.axis_index("c") + dc, 2),
        "zh": lax.div(z, 4),
        "y": lax.rem(lax.axis_index("y") + dy + 4, 4),
    }


def kernel(
    q_hbm, p_hbm, pos_hbm, oq, op,
    q, p, pos, qb, pb, posb, sc, sg, st,
    da, db, own_a, own_b, ra, rb, s2a, s2b, r2a, r2b, zs, zr,
    dps, dpr, sf, rf, sy, ry,
    ssem, rsem, isem,
):
    x, y, c, zl, zh = (lax.axis_index(a) for a in ("x", "y", "c", "zl", "zh"))
    oc = 1 - c
    oz = 1 - zh
    arrivals, departures, leaving = {}, {}, {}

    def send(src, dst, tag, out=None, **where):
        out = tag if out is None else out
        copy = pltpu.make_async_remote_copy(
            src_ref=src, dst_ref=dst,
            send_sem=ssem.at[departures.setdefault(out, len(departures))],
            recv_sem=rsem.at[arrivals.setdefault(tag, len(arrivals))],
            device_id=place(**where), device_id_type=pl.DeviceIdType.MESH,
        )
        copy.start()
        leaving.setdefault(out, []).append(dst)

    def arrived(tag, ref):
        pltpu.make_async_copy(ref, ref, rsem.at[arrivals[tag]]).wait()

    def left(out, ref):
        pltpu.make_async_copy(ref, ref, ssem.at[departures[out]]).wait()

    def half_of(dz):
        return lax.div(lax.rem(zh * 4 + zl + dz, 8), 4)

    plane = [(dx, dy) for dx in range(4) for dy in range(4) if dx or dy]
    peers = [dict(dx=dx, dy=dy) for dx, dy in plane]
    peers += [dict(dz=1), dict(dz=-1), dict(dz=4), dict(dc=1)]
    inputs = [
        pltpu.make_async_copy(a, b, isem.at[k]) for k, (a, b) in enumerate(((q_hbm, q), (p_hbm, p), (pos_hbm, pos)))
    ]
    for copy in inputs:
        copy.start()
    barrier = pltpu.get_barrier_semaphore()
    for where in peers:
        pl.semaphore_signal(barrier, inc=1, device_id=place(**where), device_id_type=pl.DeviceIdType.MESH)
    pl.semaphore_wait(barrier, len(peers))

    for copy in inputs:
        copy.wait()

    mine = pl.ds(pl.multiple_of(c * QUARTER, 16), QUARTER)
    send(q.at[pl.ds(oz * 2, 2)], qb.at[0, zh, :, pl.ds(0, QUARTER)], "swap", dz=4)
    for d in (1, 3, 2):
        rows = pl.ds(pl.multiple_of(lax.rem(y + d, 4) * QUARTER, 16), QUARTER)
        send(p.at[rows], pb.at[-d % 4, zh, mine], ("spread", -d % 4), "spread", dy=d)

    def share(src, h, tag):
        for d in (1, 3, 2):
            send(src, qb.at[-d % 4, h, :, pl.ds(0, QUARTER)], ("y", -d % 4, tag), ("share", tag), dy=d)
            send(src, qb.at[0, h, :, pl.ds((-d % 4) * QUARTER, QUARTER)], ("x", -d % 4, tag), ("share", tag), dx=d)

    share(q.at[pl.ds(zh * 2, 2)], zh, 0)
    for d in (1, 3, 2):
        send(pos, posb.at[-d % 4], "pos", dx=d)
    for g in (0, 1):
        qb[0, zh, g, 0:QUARTER, :] = q[zh * 2 + g]
    posb[0] = pos[...]
    pb[0, zh, mine, :] = p[pl.ds(pl.multiple_of(y * QUARTER, 16), QUARTER), :]

    def piece(dz, sub):
        rows = pl.ds(pl.multiple_of((dz % 4) * 2 * QUARTER + c * QUARTER, 16), QUARTER)
        ys = pl.ds(0, 4) if sub is None else pl.ds(sub * 2, 2)
        return ys, half_of(dz), rows

    def pass_on(dz, sub, step):
        ys, h, rows = piece(dz, sub)
        to = (dz - step) % 8
        to_rows = pl.ds(pl.multiple_of((to % 4) * 2 * QUARTER + c * QUARTER, 16), QUARTER)
        send(pb.at[ys, h, rows], pb.at[ys, h, to_rows], ("ring", to, sub), "ring", dz=step)

    def ring_arrived(dz, sub):
        arrived(("ring", dz, sub), pb.at[pl.ds(0, 2), 0, pl.ds(0, QUARTER)])

    def to_core(dz):
        ys, h, rows = piece(dz, None)
        send(pb.at[ys, h, rows], pb.at[ys, h, rows], ("core", dz), "core", dc=1)

    def core_arrived(*dzs):
        for dz in dzs:
            arrived(("core", dz), pb.at[:, 0, pl.ds(0, QUARTER)])

    def spread_arrived(*ds):
        for d in ds:
            arrived(("spread", d), pb.at[0, 0, pl.ds(0, QUARTER)])

    def groups_of(groups):
        return pl.ds(0, 2) if groups == "both" else pl.ds(groups, 1)

    def spread_y(k, tag, h, groups):
        gs, rows = groups_of(groups), pl.ds(0, EIGHTH)
        for d in (1, 3, 2):
            to_rows = pl.ds((-d % 4) * QUARTER, EIGHTH)
            send(qb.at[k, h, gs, rows], qb.at[k, h, gs, to_rows], ("second", tag, groups), dx=d)

    def spread_x(k, tag, h, groups):
        gs, rows = groups_of(groups), pl.ds(k * QUARTER + EIGHTH, EIGHTH)
        for d in (1, 3, 2):
            send(qb.at[0, h, gs, rows], qb.at[-d % 4, h, gs, rows], ("second", tag, groups), dy=d)

    def share_arrived(way, k, tag):
        arrived((way, k, tag), qb.at[0, 0, :, pl.ds(0, QUARTER)])

    def second_arrived(tag, groups):
        arrived(("second", tag, groups), qb.at[pl.ds(0, 3), 0, groups_of(groups), pl.ds(0, 576)])

    def hop(n):
        for sub in (0, 1):
            for dz, step in ((n, -1), (8 - n, 1)):
                ring_arrived(dz, sub)
                if n < 3 or (sub == 0) == (step == -1):
                    pass_on(dz, sub, step)
        to_core(n)
        to_core(8 - n)

    spread_arrived(1)
    pass_on(0, 0, 1)
    pass_on(0, 0, -1)
    spread_arrived(3, 2)
    pass_on(0, 1, 1)
    pass_on(0, 1, -1)
    to_core(0)
    share_arrived("x", 1, 0)
    spread_x(1, 0, zh, "both")
    share_arrived("y", 1, 0)
    spread_y(1, 0, zh, "both")
    arrived("swap", qb.at[0, 0, :, pl.ds(0, QUARTER)])
    share(qb.at[0, oz, :, pl.ds(0, QUARTER)], oz, 1)
    for k in (3, 2):
        share_arrived("x", k, 0)
        spread_x(k, 0, zh, "both")
        share_arrived("y", k, 0)
        spread_y(k, 0, zh, "both")
    hop(1)
    hop(2)
    for k in (1, 3, 2):
        share_arrived("x", k, 1)
        share_arrived("y", k, 1)
    for g in (0, 1):
        for k in (1, 3, 2):
            spread_x(k, 1, oz, g)
            spread_y(k, 1, oz, g)
    hop(3)
    arrived("pos", posb.at[pl.ds(1, 3)])
    second_arrived(0, "both")
    second_arrived(1, 0)

    def wide(ref, *at):
        return jnp.concatenate([ref[(k, h, *at)] for k in range(4) for h in range(2)], axis=1)

    best = {0: None, 1: None}

    def scores(g, n):
        rows = slice(n * HALF, (n + 1) * HALF)
        sc[g, rows, :] = lax.dot_general(wide(pb, rows), wide(qb, g), NT, preferred_element_type=F32) * SCALE

    def tally(g, n):
        s = sc[g, n * HALF : (n + 1) * HALF, :]
        high = jnp.max(s, axis=0, keepdims=True)
        if best[g] is None:
            best[g] = high, jnp.sum(jnp.exp(s - high), axis=0, keepdims=True)
        else:
            top, total = best[g]
            higher = jnp.maximum(top, high)
            total = total * jnp.exp(top - higher) + jnp.sum(jnp.exp(s - higher), axis=0, keepdims=True)
            best[g] = higher, total

    def publish(g):
        top, total = best[g]
        for i in range(4):
            st[g, 0, i, 0:1, :] = top[:, i * QUARTER : (i + 1) * QUARTER]
            st[g, 0, i, 1:2, :] = total[:, i * QUARTER : (i + 1) * QUARTER]
        for dx, dy in plane:
            send(st.at[g, 0], st.at[g, (-dx % 4) * 4 + (-dy % 4)], ("stats", g), dx=dx, dy=dy)

    core_arrived(2, 6)
    scores(0, 2)
    core_arrived(1, 5, 3, 7)
    scores(0, 1)
    tally(0, 2)
    scores(0, 3)
    tally(0, 1)
    for sub in (0, 1):
        ring_arrived(4, sub)
    to_core(4)
    second_arrived(1, 1)
    scores(1, 2)
    tally(0, 3)
    core_arrived(0, 4)
    scores(0, 0)
    tally(1, 2)
    scores(1, 1)
    tally(0, 0)
    publish(0)
    scores(1, 3)
    tally(1, 1)
    scores(1, 0)
    tally(1, 3)
    tally(1, 0)
    publish(1)

    def normalise(g):
        arrived(("stats", g), st.at[g, pl.ds(1, 15)])
        logs = []
        for i in range(4):
            pairs = [(k, (i - k // 4) % 4) for k in range(16)]
            tops = [st[g, k, n, 0:1, :] for k, n in pairs]
            high = functools.reduce(jnp.maximum, tops)
            total = sum(st[g, k, n, 1:2, :] * jnp.exp(t - high) for (k, n), t in zip(pairs, tops))
            logs.append(high + jnp.log(total))
        log_total = jnp.concatenate(logs, axis=1)
        targets = []
        for i in range(4):
            three = jnp.concatenate([posb[i, pl.ds(zh * 3 + t, 1), :] for t in range(3)], axis=1)
            targets.append(three[:, g * QUARTER : (g + 1) * QUARTER])
        targets = jnp.concatenate(targets, axis=1)

        def normal(j, carry, g=g, log_total=log_total, targets=targets):
            rows = pl.ds(pl.multiple_of(j * QUARTER, 16), QUARTER)
            owner = (lax.rem(zl + lax.div(j, 2), 4) * 4 + x) * 2 + lax.rem(j, 2)
            ids = lax.broadcasted_iota(jnp.int32, (QUARTER, GROUP), 0) + (owner * 768 + y * QUARTER)
            e = jnp.exp(sc[g, rows, :] - log_total)
            sg[g, rows, :] = jnp.where(ids == targets, e - 1.0, e).astype(BF16)
            return carry

        lax.fori_loop(0, 8, normal, 0)

    def query_gradients(g):
        r = lax.dot_general(sg[g], wide(pb), TN, preferred_element_type=F32)
        for i in (1, 3, 2, 0):
            for k in range(4):
                rows, columns = slice(i * QUARTER, i * QUARTER + EIGHTH), slice(k * 256, (k + 1) * 256)
                if i:
                    da[g, i, k] = r[rows, columns].astype(BF16)
                else:
                    own_a[g, k] = r[rows, columns]
            if i:
                send(da.at[g, i], ra.at[g, -i % 4], ("a", g), dx=i)
        for k in (1, 3, 2, 0):
            for i in range(4):
                rows, columns = slice(i * QUARTER + EIGHTH, (i + 1) * QUARTER), slice(k * 256, (k + 1) * 256)
                if k:
                    db[g, k, i] = r[rows, columns].astype(BF16)
                else:
                    own_b[g, i] = r[rows, columns]
            if k:
                send(db.at[g, k], rb.at[g, -k % 4], ("b", g), dy=k)

    def passages(s):
        rows = slice(s * HALF, (s + 1) * HALF)
        r = jnp.dot(
            jnp.concatenate([sg[g, rows, :] for g in range(2)], axis=1),
            jnp.concatenate([wide(qb, g) for g in range(2)], axis=0),
            preferred_element_type=F32,
        )
        for k in range(4):
            for i in range(2):
                for h in range(2):
                    column = k * 256 + h * 128
                    dps[s, i, h, k] = r[i * QUARTER : (i + 1) * QUARTER, column : column + 128]
        send(dps.at[s, oc], dpr.at[s], ("half", s), "half", dc=1)

    def half_arrived(*ss):
        for s in ss:
            arrived(("half", s), dpr.at[s])

    def both(dz, k):
        h = half_of(dz)
        return dps[dz % 4, c, h, k] + dpr[dz % 4, h, k]

    def add_on(way, n, sub, first=False):
        dz = (4 - n) if way == 0 else (4 + n)
        for i in range(2):
            v = both(dz, sub * 2 + i)
            if not first:
                v = v + rf[way, n, sub, i].astype(F32)
            sf[way, n, sub, i] = v.astype(BF16)
        send(sf.at[way, n, sub], rf.at[way, n + 1, sub], ("sum", way, n + 1, sub), "sum", dz=1 - 2 * way)

    def sum_arrived(way, n, sub):
        arrived(("sum", way, n, sub), rf.at[way, n, sub])

    def step(n):
        for way, sub in ((0, 1), (1, 0), (0, 0), (1, 1)):
            sum_arrived(way, n, sub)
            add_on(way, n, sub)

    def second_stage(g):
        arrived(("a", g), ra.at[g, pl.ds(1, 3)])
        arrived(("b", g), rb.at[g, pl.ds(1, 3)])
        for k in (1, 3, 2, 0):
            va = own_a[g, k] + sum(ra[g, i, k].astype(F32) for i in (1, 2, 3))
            vb = own_b[g, k] + sum(rb[g, i, k].astype(F32) for i in (1, 2, 3))
            if k:
                s2a[g, k] = va.astype(BF16)
                send(s2a.at[g, k], r2a.at[g, -k % 4], ("a2", g), dy=k)
                s2b[g, k] = vb.astype(BF16)
                send(s2b.at[g, k], r2b.at[g, -k % 4], ("b2", g), dx=k)
            else:
                own_a[g, 0] = va
                own_b[g, 0] = vb

    def third_stage(g):
        arrived(("a2", g), r2a.at[g, pl.ds(1, 3)])
        arrived(("b2", g), r2b.at[g, pl.ds(1, 3)])
        fa = own_a[g, 0] + sum(r2a[g, k].astype(F32) for k in (1, 2, 3))
        fb = own_b[g, 0] + sum(r2b[g, k].astype(F32) for k in (1, 2, 3))
        for h in range(2):
            zs[h, g, 0:EIGHTH, :] = fa[:, h * 128 : (h + 1) * 128].astype(BF16)
            zs[h, g, EIGHTH:QUARTER, :] = fb[:, h * 128 : (h + 1) * 128].astype(BF16)
        send(zs.at[oz, g], zr.at[g], ("last", g), dz=4)
        oq[pl.ds(pl.multiple_of(zh * HALF + g * QUARTER, 16), QUARTER), :] = zs[zh, g]

    normalise(0)
    query_gradients(0)
    normalise(1)
    passages(0)
    passages(3)
    half_arrived(0)
    add_on(0, 0, 0, True)
    add_on(1, 0, 1, True)
    passages(1)
    half_arrived(3)
    add_on(0, 1, 1, True)
    passages(2)
    half_arrived(1)
    add_on(1, 1, 0, True)
    query_gradients(1)
    for way, sub in ((0, 0), (1, 1)):
        sum_arrived(way, 1, sub)
        add_on(way, 1, sub)
    half_arrived(2)
    second_stage(0)
    step(2)
    second_stage(1)
    third_stage(0)
    step(3)
    third_stage(1)

    for way, sub in ((0, 1), (1, 0), (0, 0), (1, 1)):
        sum_arrived(way, 4, sub)
    for k in (1, 3, 2, 0):
        v = both(0, k) + rf[0, 4, k // 2, k % 2].astype(F32) + rf[1, 4, k // 2, k % 2].astype(F32)
        if k:
            sy[k] = v.astype(BF16)
            send(sy.at[k], ry.at[-k % 4], "widths", dy=k)
        else:
            op[pl.ds(pl.multiple_of(y * QUARTER, 16), QUARTER), :] = v.astype(BF16)
    arrived("widths", ry.at[pl.ds(1, 3)])
    for k in (1, 2, 3):
        op[pl.ds(pl.multiple_of(lax.rem(y + k, 4) * QUARTER, 16), QUARTER), :] = ry[k]
    for g in (0, 1):
        arrived(("last", g), zr.at[g])
        oq[pl.ds(pl.multiple_of(oz * HALF + g * QUARTER, 16), QUARTER), :] = zr[g]
    rest = {
        "spread": pb.at[pl.ds(0, 3), 0, pl.ds(0, QUARTER)],
        "ring": pb.at[:, 0, pl.ds(0, 1344)],
        "core": pb.at[:, 0],
        ("share", 0): qb.at[pl.ds(0, 3), 0, 0],
        ("share", 1): qb.at[pl.ds(0, 3), 0, 0],
        "pos": posb.at[pl.ds(1, 3)],
        ("second", 0, "both"): qb.at[pl.ds(0, 3), 0, :, pl.ds(0, 576)],
        ("second", 1, 0): qb.at[pl.ds(0, 3), 0, pl.ds(0, 1), pl.ds(0, 576)],
        ("second", 1, 1): qb.at[pl.ds(0, 3), 0, pl.ds(0, 1), pl.ds(0, 576)],
        "half": dpr,
        "sum": pb.at[:, 0, pl.ds(0, 1344)],
        "widths": ry.at[pl.ds(1, 3)],
    }
    for g in (0, 1):
        rest["stats", g] = st.at[g, pl.ds(1, 15)]
        rest["a", g], rest["b", g] = ra.at[g, pl.ds(1, 3)], rb.at[g, pl.ds(1, 3)]
        rest["a2", g], rest["b2", g] = r2a.at[g, pl.ds(1, 3)], r2b.at[g, pl.ds(1, 3)]
    for out, dsts in leaving.items():
        ref = dsts[0] if len(dsts) == 1 else rest[out]
        size = lambda r: math.prod(r.shape) * r.dtype.itemsize
        assert size(ref) == sum(size(d) for d in dsts), out
        left(out, ref)
    assert (len(arrivals), len(departures)) == (ARRIVALS, DEPARTURES), (len(arrivals), len(departures))


def local(queries, passages, positive):
    vmem = pl.BlockSpec(memory_space=pltpu.VMEM)
    shapes = [
        ((4, QUARTER, 128), BF16),
        ((768, 128), BF16),
        ((6, 128), jnp.int32),
        ((4, 2, 2, GROUP, 128), BF16),
        ((4, 2, BLOCK, 128), BF16),
        ((4, 6, 128), jnp.int32),
        ((2, BLOCK, GROUP), F32),
        ((2, BLOCK, GROUP), BF16),
        ((2, 16, 4, 2, QUARTER), F32),
        ((2, 4, 4, EIGHTH, 256), BF16),
        ((2, 4, 4, EIGHTH, 256), BF16),
        ((2, 4, EIGHTH, 256), F32),
        ((2, 4, EIGHTH, 256), F32),
        ((2, 4, 4, EIGHTH, 256), BF16),
        ((2, 4, 4, EIGHTH, 256), BF16),
        ((2, 4, EIGHTH, 256), BF16),
        ((2, 4, EIGHTH, 256), BF16),
        ((2, 4, EIGHTH, 256), BF16),
        ((2, 4, EIGHTH, 256), BF16),
        ((2, 2, QUARTER, 128), BF16),
        ((2, QUARTER, 128), BF16),
        ((4, 2, 2, 4, QUARTER, 128), F32),
        ((4, 2, 4, QUARTER, 128), F32),
        ((2, 4, 2, 2, QUARTER, 128), BF16),
        ((2, 5, 2, 2, QUARTER, 128), BF16),
        ((4, QUARTER, 128), BF16),
        ((4, QUARTER, 128), BF16),
    ]
    return pl.pallas_call(
        kernel,
        out_shape=(pltpu.VMEM((768, 128), BF16), pltpu.VMEM((768, 128), BF16)),
        in_specs=[pl.BlockSpec(memory_space=pl.ANY)] * 3,
        out_specs=(vmem, vmem),
        scratch_shapes=[pltpu.VMEM(s, t) for s, t in shapes]
        + [pltpu.SemaphoreType.DMA((n,)) for n in (DEPARTURES, ARRIVALS, 3)],
        compiler_params=pltpu.CompilerParams(
            collective_id=0, has_side_effects=True, vmem_limit_bytes=62 * 2**20
        ),
    )(queries.reshape(4, QUARTER, 128), passages, positive.reshape(6, 128))


def solution(mesh):
    finer = Mesh(mesh.devices.reshape(4, 4, 2, 2, 4), ("zl", "x", "c", "zh", "y"))
    dp, mp = ("zl", "x", "c"), ("zh", "y")
    return jax.shard_map(
        local,
        mesh=finer,
        in_specs=(P(dp, mp), P(dp, mp), P(dp)),
        out_specs=(P(dp, mp), P(dp, mp)),
        check_vma=False,
    )
```

time: 100 us -> 88.1 us (0.88)
  Pallas kernels: 95.7 us -> 86 us
  local copies, waits for them, and re-layouts: 3.69 us -> 1.36 us
    pallas_call x1, Pallas kernels: 95.7 us -> 86 us  [local(): pl.pallas_call(kernel, out_shape=(pltpu.VMEM((768, 128), BF16), pltpu.VME...]
    reshape x1 -> x0, local copies, waits for them, and re-layouts: 1.36 us -> none  [local(): positive.reshape(2, 2, 1, QUARTER)]
    unnamed x4 -> x2, local copies, waits for them, and re-layouts: 2.34 us -> 1.36 us
where the time goes in v2:
time: 88.1 us; the launch traced here: 88 us
  Pallas kernels  86 us (98%)
  local copies, waits for them, and re-layouts  1.36 us (2%)
    pallas_call x1, Pallas kernels, local(): pl.pallas_call(kernel, out_shape=(pltpu.VMEM((768, 128), BF16), pltpu.VME...  86 us

profile of v2, /device:TPU:8, one launch (start us, length us, event | category | flops | bytes accessed | tf_op | source)
XLA Modules:
  0.0 88.0 jit_solution(13218662953202505992)
XLA Ops:
  0.6 86.0 %shard_map.50 = (bf16[768,128]{1,0:T(8,128)(2,1)S(1)}, bf16[768,128]{1,0:T(8,128)(2,1)S(1)}) custom-call(bf16[4,192,128]{2,1,0:T(8,128)(2,1)} %bitcast.2, bf16[768,128]{1,0:T(8,128)(2,1)} %p_hbm.1, s32[6,128]{1,0:T(8,128)} %bitcast.3), custom_call_target="tpu_custom_call" | custom-call | tf_op jit(solution)/shard_map/pallas_call | solution.py:452
  86.6 0.7 copy.7
  87.3 0.7 copy.8

commit v3 on v2

--- a/solution.py
+++ b/solution.py
@@ -215,23 +215,23 @@
 
     core_arrived(2, 6)
     scores(0, 2)
+    for sub in (0, 1):
+        ring_arrived(4, sub)
+    to_core(4)
     core_arrived(1, 5, 3, 7)
     scores(0, 1)
     tally(0, 2)
     scores(0, 3)
     tally(0, 1)
-    for sub in (0, 1):
-        ring_arrived(4, sub)
-    to_core(4)
     second_arrived(1, 1)
     scores(1, 2)
     tally(0, 3)
     core_arrived(0, 4)
     scores(0, 0)
     tally(1, 2)
-    scores(1, 1)
     tally(0, 0)
     publish(0)
+    scores(1, 1)
     scores(1, 3)
     tally(1, 1)
     scores(1, 0)
@@ -239,7 +239,9 @@
     tally(1, 0)
     publish(1)
 
-    def normalise(g):
+    logs_of, targets_of = {}, {}
+
+    def normaliser(g):
         arrived(("stats", g), st.at[g, pl.ds(1, 15)])
         logs = []
         for i in range(4):
@@ -248,43 +250,51 @@
             high = functools.reduce(jnp.maximum, tops)
             total = sum(st[g, k, n, 1:2, :] * jnp.exp(t - high) for (k, n), t in zip(pairs, tops))
             logs.append(high + jnp.log(total))
-        log_total = jnp.concatenate(logs, axis=1)
         targets = []
         for i in range(4):
             three = jnp.concatenate([posb[i, pl.ds(zh * 3 + t, 1), :] for t in range(3)], axis=1)
             targets.append(three[:, g * QUARTER : (g + 1) * QUARTER])
-        targets = jnp.concatenate(targets, axis=1)
-
-        def normal(j, carry, g=g, log_total=log_total, targets=targets):
+        for half in (0, 1):
+            two = slice(half * 2, half * 2 + 2)
+            logs_of[g, half] = jnp.concatenate(logs[two], axis=1)
+            targets_of[g, half] = jnp.concatenate(targets[two], axis=1)
+
+    def normalise(g, half):
+        columns = slice(half * HALF, (half + 1) * HALF)
+        log_total, targets = logs_of[g, half], targets_of[g, half]
+
+        def normal(j, carry):
             rows = pl.ds(pl.multiple_of(j * QUARTER, 16), QUARTER)
             owner = (lax.rem(zl + lax.div(j, 2), 4) * 4 + x) * 2 + lax.rem(j, 2)
-            ids = lax.broadcasted_iota(jnp.int32, (QUARTER, GROUP), 0) + (owner * 768 + y * QUARTER)
-            e = jnp.exp(sc[g, rows, :] - log_total)
-            sg[g, rows, :] = jnp.where(ids == targets, e - 1.0, e).astype(BF16)
+            ids = lax.broadcasted_iota(jnp.int32, (QUARTER, HALF), 0) + (owner * 768 + y * QUARTER)
+            e = jnp.exp(sc[g, rows, columns] - log_total)
+            sg[g, rows, columns] = jnp.where(ids == targets, e - 1.0, e).astype(BF16)
             return carry
 
         lax.fori_loop(0, 8, normal, 0)
 
-    def query_gradients(g):
-        r = lax.dot_general(sg[g], wide(pb), TN, preferred_element_type=F32)
-        for i in (1, 3, 2, 0):
-            for k in range(4):
-                rows, columns = slice(i * QUARTER, i * QUARTER + EIGHTH), slice(k * 256, (k + 1) * 256)
-                if i:
-                    da[g, i, k] = r[rows, columns].astype(BF16)
+    def query_gradients(g, half):
+        r = lax.dot_general(
+            sg[g, :, half * HALF : (half + 1) * HALF], wide(pb), TN, preferred_element_type=F32
+        )
+        pair = pl.ds(half * 2, 2)
+        for k in (1, 3, 2, 0):
+            columns = slice(k * 256, (k + 1) * 256)
+            for i in range(2):
+                part_a = r[i * QUARTER : i * QUARTER + EIGHTH, columns]
+                part_b = r[i * QUARTER + EIGHTH : (i + 1) * QUARTER, columns]
+                if half or i:
+                    da[g, half * 2 + i, k] = part_a.astype(BF16)
                 else:
-                    own_a[g, k] = r[rows, columns]
-            if i:
-                send(da.at[g, i], ra.at[g, -i % 4], ("a", g), dx=i)
-        for k in (1, 3, 2, 0):
-            for i in range(4):
-                rows, columns = slice(i * QUARTER + EIGHTH, (i + 1) * QUARTER), slice(k * 256, (k + 1) * 256)
+                    own_a[g, k] = part_a
                 if k:
-                    db[g, k, i] = r[rows, columns].astype(BF16)
+                    db[g, k, half * 2 + i] = part_b.astype(BF16)
                 else:
-                    own_b[g, i] = r[rows, columns]
+                    own_b[g, half * 2 + i] = part_b
             if k:
-                send(db.at[g, k], rb.at[g, -k % 4], ("b", g), dy=k)
+                send(db.at[g, k, pair], rb.at[g, -k % 4, pair], ("b", g), dy=k)
+        for i in (3, 2) if half else (1,):
+            send(da.at[g, i], ra.at[g, -i % 4], ("a", g), dx=i)
 
     def passages(s):
         rows = slice(s * HALF, (s + 1) * HALF)
@@ -351,30 +361,35 @@
         send(zs.at[oz, g], zr.at[g], ("last", g), dz=4)
         oq[pl.ds(pl.multiple_of(zh * HALF + g * QUARTER, 16), QUARTER), :] = zs[zh, g]
 
-    normalise(0)
-    query_gradients(0)
-    normalise(1)
+    normaliser(0)
+    for half in (1, 0):
+        normalise(0, half)
+        query_gradients(0, half)
+    normaliser(1)
+    normalise(1, 1)
+    normalise(1, 0)
     passages(0)
     passages(3)
     half_arrived(0)
     add_on(0, 0, 0, True)
     add_on(1, 0, 1, True)
-    passages(1)
+    query_gradients(1, 1)
     half_arrived(3)
     add_on(0, 1, 1, True)
+    query_gradients(1, 0)
+    passages(1)
     passages(2)
     half_arrived(1)
     add_on(1, 1, 0, True)
-    query_gradients(1)
     for way, sub in ((0, 0), (1, 1)):
         sum_arrived(way, 1, sub)
         add_on(way, 1, sub)
     half_arrived(2)
     second_stage(0)
     step(2)
+    step(3)
     second_stage(1)
     third_stage(0)
-    step(3)
     third_stage(1)
 
     for way, sub in ((0, 1), (1, 0), (0, 0), (1, 1)):

time: 88.1 us -> 83.1 us (0.943)
  Pallas kernels: 86 us -> 80.7 us
    pallas_call x1, Pallas kernels: 86 us -> 80.7 us  [local(): pl.pallas_call(kernel, out_shape=(pltpu.VMEM((768, 128), BF16), pltpu.VME...]
where the time goes in v3:
time: 83.1 us; the launch traced here: 82.7 us
  Pallas kernels  80.7 us (97%)
  local copies, waits for them, and re-layouts  1.36 us (2%)
    pallas_call x1, Pallas kernels, local(): pl.pallas_call(kernel, out_shape=(pltpu.VMEM((768, 128), BF16), pltpu.VME...  80.7 us

profile of v3, /device:TPU:8, one launch (start us, length us, event | category | flops | bytes accessed | tf_op | source)
XLA Modules:
  0.0 82.7 jit_solution(1892921879716421575)
XLA Ops:
  0.6 80.7 %shard_map.50 = (bf16[768,128]{1,0:T(8,128)(2,1)S(1)}, bf16[768,128]{1,0:T(8,128)(2,1)S(1)}) custom-call(bf16[4,192,128]{2,1,0:T(8,128)(2,1)} %bitcast.2, bf16[768,128]{1,0:T(8,128)(2,1)} %p_hbm.1, s32[6,128]{1,0:T(8,128)} %bitcast.3), custom_call_target="tpu_custom_call" | custom-call | tf_op jit(solution)/shard_map/pallas_call | solution.py:467
  81.4 0.7 copy.7
  82.1 0.7 copy.8

commit v4 on v3

--- a/solution.py
+++ b/solution.py
@@ -223,15 +223,15 @@
     tally(0, 2)
     scores(0, 3)
     tally(0, 1)
+    core_arrived(0, 4)
+    scores(0, 0)
+    tally(0, 3)
+    tally(0, 0)
+    publish(0)
     second_arrived(1, 1)
     scores(1, 2)
-    tally(0, 3)
-    core_arrived(0, 4)
-    scores(0, 0)
+    scores(1, 1)
     tally(1, 2)
-    tally(0, 0)
-    publish(0)
-    scores(1, 1)
     scores(1, 3)
     tally(1, 1)
     scores(1, 0)
@@ -362,45 +362,50 @@
         oq[pl.ds(pl.multiple_of(zh * HALF + g * QUARTER, 16), QUARTER), :] = zs[zh, g]
 
     normaliser(0)
-    for half in (1, 0):
-        normalise(0, half)
-        query_gradients(0, half)
+    normalise(0, 1)
+    query_gradients(0, 1)
+    normalise(0, 0)
     normaliser(1)
     normalise(1, 1)
     normalise(1, 0)
     passages(0)
+    query_gradients(0, 0)
     passages(3)
     half_arrived(0)
     add_on(0, 0, 0, True)
     add_on(1, 0, 1, True)
+    passages(1)
     query_gradients(1, 1)
-    half_arrived(3)
+    half_arrived(3, 1)
     add_on(0, 1, 1, True)
-    query_gradients(1, 0)
-    passages(1)
+    add_on(1, 1, 0, True)
     passages(2)
-    half_arrived(1)
-    add_on(1, 1, 0, True)
     for way, sub in ((0, 0), (1, 1)):
         sum_arrived(way, 1, sub)
         add_on(way, 1, sub)
+    query_gradients(1, 0)
+    second_stage(0)
     half_arrived(2)
-    second_stage(0)
     step(2)
     step(3)
     second_stage(1)
     third_stage(0)
     third_stage(1)
 
-    for way, sub in ((0, 1), (1, 0), (0, 0), (1, 1)):
-        sum_arrived(way, 4, sub)
-    for k in (1, 3, 2, 0):
+    def last_step(k):
         v = both(0, k) + rf[0, 4, k // 2, k % 2].astype(F32) + rf[1, 4, k // 2, k % 2].astype(F32)
         if k:
             sy[k] = v.astype(BF16)
             send(sy.at[k], ry.at[-k % 4], "widths", dy=k)
         else:
             op[pl.ds(pl.multiple_of(y * QUARTER, 16), QUARTER), :] = v.astype(BF16)
+
+    for way, sub in ((0, 1), (1, 0), (0, 0)):
+        sum_arrived(way, 4, sub)
+    last_step(1)
+    sum_arrived(1, 4, 1)
+    for k in (3, 2, 0):
+        last_step(k)
     arrived("widths", ry.at[pl.ds(1, 3)])
     for k in (1, 2, 3):
         op[pl.ds(pl.multiple_of(lax.rem(y + k, 4) * QUARTER, 16), QUARTER), :] = ry[k]

time: 83.1 us -> 78.9 us (0.949)
  Pallas kernels: 80.7 us -> 76.8 us
    pallas_call x1, Pallas kernels: 80.7 us -> 76.8 us  [local(): pl.pallas_call(kernel, out_shape=(pltpu.VMEM((768, 128), BF16), pltpu.VME...]
where the time goes in v4:
time: 78.9 us; the launch traced here: 78.8 us
  Pallas kernels  76.8 us (97%)
  local copies, waits for them, and re-layouts  1.36 us (2%)
    pallas_call x1, Pallas kernels, local(): pl.pallas_call(kernel, out_shape=(pltpu.VMEM((768, 128), BF16), pltpu.VME...  76.8 us

profile of v4, /device:TPU:8, one launch (start us, length us, event | category | flops | bytes accessed | tf_op | source)
XLA Modules:
  0.0 78.8 jit_solution(8654149521958714704)
XLA Ops:
  0.6 76.8 %shard_map.50 = (bf16[768,128]{1,0:T(8,128)(2,1)S(1)}, bf16[768,128]{1,0:T(8,128)(2,1)S(1)}) custom-call(bf16[4,192,128]{2,1,0:T(8,128)(2,1)} %bitcast.2, bf16[768,128]{1,0:T(8,128)(2,1)} %p_hbm.1, s32[6,128]{1,0:T(8,128)} %bitcast.3), custom_call_target="tpu_custom_call" | custom-call | tf_op jit(solution)/shard_map/pallas_call | solution.py:472
  77.5 0.7 copy.7
  78.1 0.7 copy.8

commit v5 on v4

--- a/solution.py
+++ b/solution.py
@@ -32,7 +32,7 @@
 
 
 def kernel(
-    q_hbm, p_hbm, pos_hbm, oq, op,
+    q_hbm, p_hbm, pos_hbm, out,
     q, p, pos, qb, pb, posb, sc, sg, st,
     da, db, own_a, own_b, ra, rb, s2a, s2b, r2a, r2b, zs, zr,
     dps, dpr, sf, rf, sy, ry,
@@ -359,7 +359,7 @@
             zs[h, g, 0:EIGHTH, :] = fa[:, h * 128 : (h + 1) * 128].astype(BF16)
             zs[h, g, EIGHTH:QUARTER, :] = fb[:, h * 128 : (h + 1) * 128].astype(BF16)
         send(zs.at[oz, g], zr.at[g], ("last", g), dz=4)
-        oq[pl.ds(pl.multiple_of(zh * HALF + g * QUARTER, 16), QUARTER), :] = zs[zh, g]
+        out[0, pl.ds(pl.multiple_of(zh * HALF + g * QUARTER, 16), QUARTER), :] = zs[zh, g]
 
     normaliser(0)
     normalise(0, 1)
@@ -398,7 +398,7 @@
             sy[k] = v.astype(BF16)
             send(sy.at[k], ry.at[-k % 4], "widths", dy=k)
         else:
-            op[pl.ds(pl.multiple_of(y * QUARTER, 16), QUARTER), :] = v.astype(BF16)
+            out[1, pl.ds(pl.multiple_of(y * QUARTER, 16), QUARTER), :] = v.astype(BF16)
 
     for way, sub in ((0, 1), (1, 0), (0, 0)):
         sum_arrived(way, 4, sub)
@@ -408,10 +408,10 @@
         last_step(k)
     arrived("widths", ry.at[pl.ds(1, 3)])
     for k in (1, 2, 3):
-        op[pl.ds(pl.multiple_of(lax.rem(y + k, 4) * QUARTER, 16), QUARTER), :] = ry[k]
+        out[1, pl.ds(pl.multiple_of(lax.rem(y + k, 4) * QUARTER, 16), QUARTER), :] = ry[k]
     for g in (0, 1):
         arrived(("last", g), zr.at[g])
-        oq[pl.ds(pl.multiple_of(oz * HALF + g * QUARTER, 16), QUARTER), :] = zr[g]
+        out[0, pl.ds(pl.multiple_of(oz * HALF + g * QUARTER, 16), QUARTER), :] = zr[g]
     rest = {
         "spread": pb.at[pl.ds(0, 3), 0, pl.ds(0, QUARTER)],
         "ring": pb.at[:, 0, pl.ds(0, 1344)],
@@ -469,17 +469,18 @@
         ((4, QUARTER, 128), BF16),
         ((4, QUARTER, 128), BF16),
     ]
-    return pl.pallas_call(
+    grads = pl.pallas_call(
         kernel,
-        out_shape=(pltpu.VMEM((768, 128), BF16), pltpu.VMEM((768, 128), BF16)),
+        out_shape=pltpu.VMEM((2, 768, 128), BF16),
         in_specs=[pl.BlockSpec(memory_space=pl.ANY)] * 3,
-        out_specs=(vmem, vmem),
+        out_specs=vmem,
         scratch_shapes=[pltpu.VMEM(s, t) for s, t in shapes]
         + [pltpu.SemaphoreType.DMA((n,)) for n in (DEPARTURES, ARRIVALS, 3)],
         compiler_params=pltpu.CompilerParams(
             collective_id=0, has_side_effects=True, vmem_limit_bytes=62 * 2**20
         ),
     )(queries.reshape(4, QUARTER, 128), passages, positive.reshape(6, 128))
+    return grads[0], grads[1]
 
 
 def solution(mesh):

time: 78.9 us -> 78.3 us (level)
    unnamed x2 -> x0, local copies, waits for them, and re-layouts: 1.36 us -> none
where the time goes in v5:
time: 78.3 us; the launch traced here: 78.2 us
  Pallas kernels  76.8 us (98%)
    pallas_call x1, Pallas kernels, local(): pl.pallas_call(kernel, out_shape=pltpu.VMEM((2, 768, 128), BF16), in_spec...  76.8 us

profile of v5, /device:TPU:8, one launch (start us, length us, event | category | flops | bytes accessed | tf_op | source)
XLA Modules:
  0.0 78.2 jit_solution(14728926384726867855)
XLA Ops:
  0.6 76.8 %shard_map.50 = bf16[2,768,128]{2,1,0:T(8,128)(2,1)S(1)} custom-call(bf16[4,192,128]{2,1,0:T(8,128)(2,1)} %bitcast.6, bf16[768,128]{1,0:T(8,128)(2,1)} %p_hbm.1, s32[6,128]{1,0:T(8,128)} %bitcast.7), custom_call_target="tpu_custom_call" | custom-call | tf_op jit(solution)/shard_map/pallas_call | solution.py:472
  77.5 0.8 slice_bitcast_fusion

commit v6 on v5

--- a/solution.py
+++ b/solution.py
@@ -223,9 +223,9 @@
     tally(0, 2)
     scores(0, 3)
     tally(0, 1)
+    tally(0, 3)
     core_arrived(0, 4)
     scores(0, 0)
-    tally(0, 3)
     tally(0, 0)
     publish(0)
     second_arrived(1, 1)

time: 78.3 us -> 78.5 us (level)
  no operation moved by 1% of the time
where the time goes in v6:
time: 78.5 us; the launch traced here: 78 us
  Pallas kernels  76.6 us (98%)
    pallas_call x1, Pallas kernels, local(): pl.pallas_call(kernel, out_shape=pltpu.VMEM((2, 768, 128), BF16), in_spec...  76.6 us

profile of v6, /device:TPU:8, one launch (start us, length us, event | category | flops | bytes accessed | tf_op | source)
XLA Modules:
  0.0 78.0 jit_solution(12636587106048651845)
XLA Ops:
  0.6 76.6 %shard_map.50 = bf16[2,768,128]{2,1,0:T(8,128)(2,1)S(1)} custom-call(bf16[4,192,128]{2,1,0:T(8,128)(2,1)} %bitcast.6, bf16[768,128]{1,0:T(8,128)(2,1)} %p_hbm.1, s32[6,128]{1,0:T(8,128)} %bitcast.7), custom_call_target="tpu_custom_call" | custom-call | tf_op jit(solution)/shard_map/pallas_call | solution.py:472
  77.2 0.8 slice_bitcast_fusion
